TPU v7x, 32 devices: a whole 2x2x4 slice. The times are simulated.
32 devices in a mesh: fft: 8 (over z, y), band: 4 (over x, core).
Axes of the slice: x: 2, y: 2, z: 4, core: 2. Of those that a mesh axis runs over, the one named last changes fastest.
Arguments:
- coefficients: bfloat16 [48, 184320], P('band', 'fft'), may hold values from -0.078125 to 0.078125
- occupations: float32 [48], P('band'), may hold values from 0.5 to 2
- columns: int32 [1280], P('fft'), may hold values from 0 to 5183
- counts: int32 [8], P('fft'), may hold values from 1 to 160, 512 in all
- plane_slot: int32 [144], replicated, may hold values from -1 to 143, as said below
Outputs:
- density: float32 [144, 144, 144], P('fft', 'band')
Inputs may be any that keep to these rules, and one draw needn't show every extreme that they name: The counts sum to 512, and one of them equals 160. `plane_slot`: every plane 0 .. 143 stands in exactly one slot; the other slots hold -1.
All inputs are finite; a program needn't handle non-finite values. No bound on the sum of `counts` on one device may be relied on, other than what follows from the above.
Results may differ from a plain program's by a relative error of at most 0.0095.
Values may be sent and summed in bfloat16 or wider, within the bound.
A program may use at most 192 MiB of HBM per device.

v0:
```python
import math

import jax
import jax.numpy as jnp
from jax import lax
from jax.sharding import PartitionSpec as P

N = 144
GB = 72


def phase_pair(freq_count, positions, grid):
    freqs = jnp.arange(freq_count, dtype=jnp.int32) - freq_count // 2
    turns = jnp.mod(freqs[:, None] * positions[None, :], grid)
    angles = turns.astype(jnp.float32) * (2.0 * math.pi / grid)
    return (jnp.cos(angles), jnp.sin(angles))


def stick_table(plane_slot):
    valid_slot = (plane_slot >= 0).astype(jnp.float32)
    cosine, sine_part = phase_pair(GB, jnp.maximum(plane_slot, 0), N)
    cosine = cosine * valid_slot[None, :]
    sine_part = sine_part * valid_slot[None, :]
    upper_rows = jnp.concatenate([cosine, sine_part], axis=1)
    lower_rows = jnp.concatenate([-sine_part, cosine], axis=1)
    return jnp.concatenate([upper_rows, lower_rows], axis=0).astype(jnp.bfloat16)


def row_table():
    cosine, sine_part = phase_pair(GB, jnp.arange(N, dtype=jnp.int32), N)
    upper_rows = jnp.concatenate([cosine, sine_part], axis=1)
    lower_rows = jnp.concatenate([-sine_part, cosine], axis=1)
    return jnp.concatenate([upper_rows, lower_rows], axis=0).astype(jnp.bfloat16)


def column_table():
    cosine, sine_part = phase_pair(GB, jnp.arange(N, dtype=jnp.int32), N)
    return jnp.concatenate([cosine.T, sine_part.T], axis=0).astype(jnp.bfloat16)


def grid_squares(received, row_pick, col_pick, row_tab, col_tab):
    bands_here, parts, planes, slot_total = received.shape
    flat_rows = bands_here * parts * planes
    by_slot = received.reshape(flat_rows, slot_total).T
    weighted = by_slot[:, :, None] * col_pick[:, None, :]
    placed = jnp.dot(
        row_pick.T, weighted.reshape(slot_total, flat_rows * GB), preferred_element_type=jnp.float32
    )
    placed = placed.reshape(GB, bands_here, parts, planes, GB)
    g_plane = (
        jnp.transpose(placed, (1, 3, 0, 2, 4))
        .reshape(bands_here, planes, GB, 2 * GB)
        .astype(jnp.bfloat16)
    )
    half_way = jnp.einsum(
        "bpgk,kj->bpgj", g_plane, row_tab, preferred_element_type=jnp.float32
    ).astype(jnp.bfloat16)
    full_grid = jnp.einsum("xg,bpgj->bpxj", col_tab, half_way, preferred_element_type=jnp.float32)
    real_part = full_grid[:, :, :N, :N] - full_grid[:, :, N:, N:]
    imag_part = full_grid[:, :, N:, :N] + full_grid[:, :, :N, N:]
    return real_part * real_part + imag_part * imag_part


def shards(coefficients, occupations, columns, counts, plane_slot):
    bands_here = coefficients.shape[0]
    coefficients = coefficients.reshape(bands_here, -1, 2 * GB)
    sticks_here = coefficients.shape[1]
    slot_count = plane_slot.shape[0]
    total_bands = bands_here * lax.axis_size("band")
    plane_tab = stick_table(plane_slot)
    row_tab = row_table()
    col_tab = column_table()
    stick_place = jnp.arange(sticks_here, dtype=jnp.int32)
    live_here = (stick_place < counts[0]).astype(jnp.bfloat16)
    coefficients = coefficients * live_here[None, :, None]
    every_column = lax.all_gather(columns, "fft", axis=0, tiled=True)
    freq_ids = jnp.arange(GB, dtype=jnp.int32)[None, :]
    row_pick = ((every_column // GB)[:, None] == freq_ids).astype(jnp.bfloat16)
    col_pick = ((every_column % GB)[:, None] == freq_ids).astype(jnp.bfloat16)
    weights = occupations / total_bands
    sticks = jnp.einsum("bsg,go->bos", coefficients, plane_tab, preferred_element_type=jnp.float32)
    outgoing = sticks.astype(jnp.bfloat16).reshape(
        coefficients.shape[0], 2, slot_count, sticks_here
    )
    squares = grid_squares(
        lax.all_to_all(outgoing, "fft", split_axis=2, concat_axis=3, tiled=True),
        row_pick,
        col_pick,
        row_tab,
        col_tab,
    )
    local_sum = jnp.einsum("b,bpxy->pxy", weights, squares)
    return lax.psum_scatter(
        local_sum.astype(jnp.bfloat16), "band", scatter_dimension=1, tiled=True
    ).astype(jnp.float32)


def solution(mesh):
    placed = (P("band", "fft"), P("band"), P("fft"), P("fft"), P())
    return jax.shard_map(
        shards, mesh=mesh, in_specs=placed, out_specs=P("fft", "band", None), check_vma=False
    )
```

profile of v0, /device:TPU:13, one launch (start us, length us, event | category | flops | bytes accessed | tf_op | source)
XLA Modules:
  0.0 323.6 jit_solution(15147241202249923715)
XLA Ops:
  6.5 0.7 broadcast_maximum_fusion
  7.2 0.7 compare_convert_fusion.1
  7.9 2.8 reshape.49
  11.4 1.3 fusion.48
  12.6 0.7 fusion.6
  13.4 1.0 copy.13
  14.4 2.6 copy.14
  17.0 5.7 %all-to-all-start = ((bf16[12,2,144,160]{3,1,0,2:T(2,128)(2,1)}), bf16[12,2,144,160]{3,1,0,2:T(2,128)(2,1)S(1)}, u32[]{:S(2)}, u32[]{:S(2)}) async-start(bf16[12,2,144,160]{3,1,0,2:T(2,128)(2,1)} %copy.14), calls=%async_computation | async-start | bytes 3538944 | tf_op jit(solution)/shard_map/all_to_all | solution.py:86
  22.7 1.2 dynamic-slice
  24.6 0.9 dynamic-update-slice
  25.5 36.1 %all-reduce = s32[1280]{0:T(1024)S(1)} all-reduce(s32[1280]{0:T(1024)S(1)} %dynamic-update-slice), channel_id=1, replica_groups=mesh['fft'=8,'band'=4] {'fft'}, use_global_device_ids=true, to_apply=%add | all-reduce | flops 1280 | bytes 10240
  61.6 1.0 cosine_convert_fusion
  62.6 0.7 fusion.11
  64.0 2.1 reshape.51
  66.0 26.9 %broadcast_multiply_fusion = bf16[1280,432,72]{0,2,1:T(8,128)(2,1)} fusion(bf16[1280,72]{0,1:T(8,128)(2,1)} %fusion.11, bf16[1280,432]{0,1:T(8,128)(2,1)S(1)} %bitcast.59), kind=kLoop, calls=%fused_computation | loop fusion | flops 39813120 | bytes 80916480 | tf_op jit(solution)/shard_map/mul | solution.py:45
  93.0 41.5 %convert_bitcast_fusion = bf16[12,18,72,2,72]{4,2,1,3,0:T(8,128)(2,1)} fusion(bf16[12,2,18,72,1280]{4,3,2,1,0:T(8,128)(2,1)} %bitcast.15, s32[1280]{0:T(1024)S(1)} %get-tuple-element.5), kind=kOutput, calls=%fused_computation.9 | convolution fusion | flops 5735420928 | bytes 84110336 | tf_op jit(solution)/shard_map/dot_general | solution.py:46
  134.5 11.3 %copy.17 = bf16[12,18,72,2,72]{2,4,3,1,0:T(8,128)(2,1)} copy(bf16[12,18,72,2,72]{4,2,1,3,0:T(8,128)(2,1)} %convert_bitcast_fusion) | data formatting | bytes 8957952 | tf_op jit(solution)/shard_map/convert_element_type | solution.py:53
  145.8 37.3 %convolution_bitcast_fusion = f32[12,18,288,288]{2,3,1,0:T(8,128)} fusion(bf16[12,18,72,144]{2,3,1,0:T(8,128)(2,1)} %bitcast.55, bf16[72,144]{1,0:T(8,128)(2,1)S(1)} %copy-done.2, bf16[72,144]{1,0:T(8,128)(2,1)S(1)} %copy-done.1, bf16[72,144]{1,0:T(8,128)(2,1)S(1)} %copy-done, bf16[144,72]{0,1:T(8,128)(2,1)S(1)} %copy-done.4, bf16[144,72]{0,1:T(8,128)(2,1)S(1)} %copy-done.3), kind=kOutput, calls=%fused_computation.1 | convolution fusion | flops 3874728960 | bytes 76246272 | tf_op jit(solution)/shard_map/xg,bpgj->bpxj/dot_general | solution.py:58
  183.1 46.4 %fusion.1 = bf16[12,18,144,144]{2,3,1,0:T(8,128)(2,1)} fusion(f32[12,18,288,288]{2,3,1,0:T(8,128)} %convolution_bitcast_fusion), kind=kLoop, calls=%fused_computation.4 | loop fusion | flops 26873856 | bytes 80621568 | tf_op jit(solution)/shard_map/add | solution.py:61
  229.5 34.0 %copy.25 = bf16[12,18,144,144]{3,0,2,1:T(8,128)(2,1)} copy(bf16[12,18,144,144]{2,3,1,0:T(8,128)(2,1)} %fusion.1) | data formatting | bytes 17915904 | tf_op jit(solution)/shard_map/add | solution.py:61
  263.5 8.6 %fusion.52 = bf16[1,18,144,144]{3,0,2,1:T(2,128)(2,1)S(1)} fusion(bf16[12,18,144,144]{3,0,2,1:T(8,128)(2,1)} %copy.25, f32[12]{0:T(128)S(1)} %copy-done.5), kind=kOutput, calls=%fused_computation.76 | convolution fusion | flops 8957964 | bytes 9704496 | tf_op jit(solution)/shard_map/b,bpxy->pxy/dot_general | solution.py:92
  272.1 1.4 copy.31
  274.7 40.1 %all-reduce.4.cloned.1.call-done = bf16[18,144,144]{2,1,0:T(8,128)(2,1)} async-done(((bf16[18,144,144]{2,1,0:T(8,128)(2,1)}), bf16[18,144,144]{2,1,0:T(8,128)(2,1)}) %all-reduce.4.cloned.1.call-update) | async-done | bytes 746512
  314.8 2.0 dynamic-slice_convert_fusion
  (23 shorter events, 1.3 us)
Async XLA Ops:
  17.0 46.4 %all-to-all-start = ((bf16[12,2,144,160]{3,1,0,2:T(2,128)(2,1)}), bf16[12,2,144,160]{3,1,0,2:T(2,128)(2,1)S(1)}, u32[]{:S(2)}, u32[]{:S(2)}) async-start(bf16[12,2,144,160]{3,1,0,2:T(2,128)(2,1)} %copy.14), calls=%async_computation | async-start | bytes 3538944 | tf_op jit(solution)/shard_map/all_to_all | solution.py:86
  22.7 292.2 %all-reduce.4.cloned.1.call-start = ((), (), s32[]{:S(2)}) async-start(), calls=%async_computation.1 | async-start | bytes 2654208
  134.5 11.3 %copy-start = (bf16[72,144]{1,0:T(8,128)(2,1)S(1)}, bf16[72,144]{1,0:T(8,128)(2,1)}, u32[]{:S(2)}) copy-start(bf16[72,144]{1,0:T(8,128)(2,1)} %get-tuple-element.12) | copy-start | bytes 62212
  134.5 11.3 %copy-start.1 = (bf16[72,144]{1,0:T(8,128)(2,1)S(1)}, bf16[72,144]{1,0:T(8,128)(2,1)}, u32[]{:S(2)}) copy-start(bf16[72,144]{1,0:T(8,128)(2,1)} %get-tuple-element.13) | copy-start | bytes 62212
  134.5 11.3 %copy-start.2 = (bf16[72,144]{1,0:T(8,128)(2,1)S(1)}, bf16[72,144]{1,0:T(8,128)(2,1)}, u32[]{:S(2)}) copy-start(bf16[72,144]{1,0:T(8,128)(2,1)} %get-tuple-element.14) | copy-start | bytes 62212
  134.5 11.3 %copy-start.3 = (bf16[144,72]{0,1:T(8,128)(2,1)S(1)}, bf16[144,72]{0,1:T(8,128)(2,1)}, u32[]{:S(2)}) copy-start(bf16[144,72]{0,1:T(8,128)(2,1)} %get-tuple-element.10) | copy-start | bytes 62212
  134.5 11.3 %copy-start.4 = (bf16[144,72]{0,1:T(8,128)(2,1)S(1)}, bf16[144,72]{0,1:T(8,128)(2,1)}, u32[]{:S(2)}) copy-start(bf16[144,72]{0,1:T(8,128)(2,1)} %get-tuple-element.11) | copy-start | bytes 62212
  229.5 34.0 %copy-start.5 = (f32[12]{0:T(128)S(1)}, f32[12]{0:T(128)}, u32[]{:S(2)}) copy-start(f32[12]{0:T(128)} %param.6) | copy-start | bytes 148
  263.5 10.0 %copy-start.6 = (u32[32]{0:T(128)S(1)}, u32[32]{0:T(128)}, u32[]{:S(2)}) copy-start(u32[32]{0:T(128)} %constant.55) | copy-start | bytes 388
Sparse Core Ops, SparseCore 0:
  273.6 41.2 all-reduce.3
where the time goes:
time: 327 us; the launch traced here: 324 us
  matrix products  88.1 us (27%)
  other arithmetic  79.7 us (24%)
  local copies, waits for them, and re-layouts  58.4 us (18%)
  waiting for transfers between devices  40.1 us (12%)
  blocking collectives  36.1 us (11%)
  between operations  15.5 us (5%)
  starting transfers between devices  5.66 us (2%)
    add x1, other arithmetic, grid_squares(): return real_part * real_part + imag_part * imag_part  46.4 us
    dot_general x1, matrix products, grid_squares(): jnp.dot(row_pick.T, weighted.reshape(slot_total, flat_rows * GB), preferr...  41.5 us
    unnamed x2, waiting for transfers between devices  40.1 us
    dot_general x1, matrix products, grid_squares(): jnp.einsum('xg,bpgj->bpxj', col_tab, half_way, preferred_element_type=jnp...  37.3 us
    unnamed x1, blocking collectives  36.1 us
    add x1, local copies, waits for them, and re-layouts, grid_squares(): return real_part * real_part + imag_part * imag_part  34 us
    mul x1, other arithmetic, grid_squares(): weighted = by_slot[:, :, None] * col_pick[:, None, :]  26.9 us
    convert_element_type x1, local copies, waits for them, and re-layouts, grid_squares(): g_plane = jnp.transpose(placed, (1, 3, 0, 2, 4)).reshape(bands_here, plan...  11.3 us
  transfers between devices with their start and end apart: 2, of which 1 were waited for; matrix products, arithmetic and copies ran while one was open for 1% of the time, Pallas kernels for 0%

commit v1 on v0

v1 whole, which is shorter than its diff:
```python
import functools
import math

import jax
import jax.numpy as jnp
from jax import lax
from jax.experimental import pallas as pl
from jax.experimental.pallas import tpu as pltpu
from jax.sharding import PartitionSpec as P

N = 144
GB = 72
LIVE_PER_DEVICE = 64
GP = 80
YP = 256
META = 8


def phase_pair(freq_count, positions, grid):
    freqs = jnp.arange(freq_count, dtype=jnp.int32) - freq_count // 2
    turns = jnp.mod(freqs[:, None] * positions[None, :], grid)
    angles = turns.astype(jnp.float32) * (2.0 * math.pi / grid)
    return (jnp.cos(angles), jnp.sin(angles))


def stick_table(plane_slot, groups):
    valid_slot = (plane_slot >= 0).astype(jnp.float32)
    cosine, sine_part = phase_pair(GB, jnp.maximum(plane_slot, 0), N)
    cosine = cosine * valid_slot[None, :]
    sine_part = sine_part * valid_slot[None, :]
    upper = jnp.stack([cosine, sine_part], axis=-1)
    lower = jnp.stack([-sine_part, cosine], axis=-1)
    return jnp.concatenate([upper, lower], axis=0).astype(jnp.bfloat16)


def row_table():
    cosine, sine_part = phase_pair(GB, jnp.arange(N, dtype=jnp.int32), N)
    pad = lambda a: jnp.pad(a, ((0, GP - GB), (0, YP - N)))
    return jnp.concatenate(
        [pad(cosine), pad(sine_part), pad(-sine_part), pad(cosine)], axis=1
    ).astype(jnp.bfloat16)


def column_table():
    cosine, sine_part = phase_pair(GB, jnp.arange(N, dtype=jnp.int32), N)
    pad = lambda a: jnp.pad(a.T, ((0, 0), (0, GP - GB)))
    upper = jnp.concatenate([pad(cosine), pad(-sine_part)], axis=1)
    lower = jnp.concatenate([pad(sine_part), pad(cosine)], axis=1)
    return jnp.concatenate([upper, lower], axis=0).astype(jnp.bfloat16)


def grid_kernel(bands, live, weights, recv, row_tab, col_tab, out, sticks, table, masked, row_hot):
    plane = pl.program_id(0)
    sources, rows, here = recv.shape
    data_rows = rows - META

    @pl.when(plane == 0)
    def _():
        total = jnp.zeros((rows, live), jnp.float32)
        offset = jnp.zeros((1, 1), jnp.float32)
        target = lax.broadcasted_iota(jnp.int32, (live, here), 0).astype(jnp.float32)
        place = lax.broadcasted_iota(jnp.int32, (live, here), 1).astype(jnp.float32)
        for source in range(sources):
            block = recv[source]
            alive = block[data_rows:, :].astype(jnp.float32)[2:3, :]
            pick = jnp.where(target == place + offset, 1.0, 0.0) * alive
            total += lax.dot_general(
                block,
                pick.astype(jnp.bfloat16),
                (((1,), (1,)), ((), ())),
                preferred_element_type=jnp.float32,
            )
            offset += jnp.sum(alive, axis=1, keepdims=True)
        sticks[...] = total[:data_rows].reshape(sticks.shape)
        meta = total[data_rows:]
        freq = lax.broadcasted_iota(jnp.int32, (GP, live), 0).astype(jnp.float32)
        row_hot[...] = jnp.where(freq == meta[0:1, :], 1.0, 0.0)
        col_hot = jnp.where(freq == meta[1:2, :], 1.0, 0.0).astype(jnp.bfloat16)
        for part in range(2):
            table[part * live : (part + 1) * live, :] = lax.dot_general(
                col_hot,
                row_tab[:, 2 * YP * part : 2 * YP * (part + 1)],
                (((0,), (0,)), ((), ())),
                preferred_element_type=jnp.float32,
            ).astype(jnp.bfloat16)

    mine = sticks[plane]
    hot = row_hot[...]
    for part in range(2):
        for band in range(bands):
            row = mine[part * bands + band : part * bands + band + 1, :]
            masked[band * GP : (band + 1) * GP, part * live : (part + 1) * live] = (
                hot * row
            ).astype(jnp.bfloat16)
    half = jnp.dot(masked[...], table[...], preferred_element_type=jnp.float32)
    half = half.astype(jnp.bfloat16)
    density = jnp.zeros((N, YP), jnp.float32)
    for band in range(bands):
        piece = half[band * GP : (band + 1) * GP, :]
        stacked = jnp.concatenate([piece[:, :YP], piece[:, YP:]], axis=0)
        wave = jnp.dot(col_tab[...], stacked, preferred_element_type=jnp.float32)
        real, imag = wave[:N], wave[N:]
        density += weights[band] * (real * real + imag * imag)
    owners, _, own_rows, _ = out.shape
    for owner in range(owners):
        out[owner, 0] = density[owner * own_rows : (owner + 1) * own_rows, :N].astype(out.dtype)


def shards(coefficients, occupations, columns, counts, plane_slot):
    bands = coefficients.shape[0]
    here = columns.shape[0]
    ways = lax.axis_size("fft")
    groups = lax.axis_size("band")
    planes = plane_slot.shape[0] // ways
    live = LIVE_PER_DEVICE * ways
    coefficients = coefficients.reshape(bands, here, 2 * GB)
    plane_tab = stick_table(plane_slot, ways)
    weights = occupations / (bands * groups)
    made = jnp.einsum(
        "gjc,bsg->jcbs", plane_tab, coefficients, preferred_element_type=jnp.float32
    ).astype(jnp.bfloat16)
    made = made.reshape(ways, planes * 2 * bands, here)
    alive = jnp.arange(here, dtype=jnp.int32) < counts[0]
    meta = jnp.stack([columns // GB, columns % GB, alive.astype(jnp.int32)]).astype(jnp.bfloat16)
    meta = jnp.pad(meta, ((0, META - 3), (0, 0)))
    outgoing = jnp.concatenate(
        [made, jnp.broadcast_to(meta[None], (ways, META, here))], axis=1
    )
    received = lax.all_to_all(outgoing, "fft", split_axis=0, concat_axis=0, tiled=True)
    rows = N // groups
    whole = pl.BlockSpec(memory_space=pltpu.VMEM)
    local = pl.pallas_call(
        functools.partial(grid_kernel, bands, live),
        grid=(planes,),
        in_specs=[pl.BlockSpec(memory_space=pltpu.SMEM), whole, whole, whole],
        out_specs=pl.BlockSpec((groups, 1, rows, N), lambda p: (0, p, 0, 0)),
        out_shape=jax.ShapeDtypeStruct((groups, planes, rows, N), jnp.bfloat16),
        scratch_shapes=[
            pltpu.VMEM((planes, 2 * bands, live), jnp.float32),
            pltpu.VMEM((2 * live, 2 * YP), jnp.bfloat16),
            pltpu.VMEM((bands * GP, 2 * live), jnp.bfloat16),
            pltpu.VMEM((GP, live), jnp.float32),
        ],
        compiler_params=pltpu.CompilerParams(vmem_limit_bytes=60 * 1024 * 1024),
        name="grid",
    )(weights, received, row_table(), column_table())
    swapped = lax.all_to_all(local, "band", split_axis=0, concat_axis=0, tiled=True)
    return jnp.sum(swapped.astype(jnp.float32), axis=0)


def solution(mesh):
    placed = (P("band", "fft"), P("band"), P("fft"), P("fft"), P())
    return jax.shard_map(
        shards, mesh=mesh, in_specs=placed, out_specs=P("fft", "band", None), check_vma=False
    )
```

time: 327 us -> 112 us (0.34)
  the two profiles are of different devices: /device:TPU:13 before, /device:TPU:0 now
where the time goes in v1:
time: 112 us
  Pallas kernels  34.9 us (31%)
  waiting for transfers between devices  28 us (25%)
  blocking collectives  22.5 us (20%)
  local copies, waits for them, and re-layouts  9.25 us (8%)
  other arithmetic  8.04 us (7%)
  starting transfers between devices  7.44 us (7%)
    pallas_call x1, Pallas kernels, shards(): pl.pallas_call(functools.partial(grid_kernel, bands, live), grid=(planes,...  34.9 us
    all_to_all x1, waiting for transfers between devices, shards(): lax.all_to_all(outgoing, 'fft', split_axis=0, concat_axis=0, tiled=True)  28 us
    all_to_all x1, blocking collectives, shards(): lax.all_to_all(local, 'band', split_axis=0, concat_axis=0, tiled=True)  22.5 us
    all_to_all x1, starting transfers between devices, shards(): lax.all_to_all(outgoing, 'fft', split_axis=0, concat_axis=0, tiled=True)  7.44 us
    reshape x1, local copies, waits for them, and re-layouts, shards(): coefficients = coefficients.reshape(bands, here, 2 * GB)  2.8 us
    reshape x1, local copies, waits for them, and re-layouts, shards(): made = made.reshape(ways, planes * 2 * bands, here)  2.3 us
  transfers between devices with their start and end apart: 1, of which 1 were waited for; matrix products, arithmetic and copies ran while one was open for 3% of the time, Pallas kernels for 0%

profile of v1, /device:TPU:0, one launch (start us, length us, event | category | flops | bytes accessed | tf_op | source)
XLA Modules:
  0.0 111.6 jit_solution(13556041126882351616)
XLA Ops:
  0.0 0.7 broadcast_maximum_fusion
  0.7 0.7 compare_convert_fusion.1
  1.4 2.8 %reshape.226 = bf16[12,160,144]{2,1,0:T(8,128)(2,1)S(1)} reshape(bf16[12,23040]{1,0:T(8,128)(2,1)} %param.5) | data formatting | bytes 1105920 | tf_op jit(solution)/shard_map/reshape | solution.py:116
  4.2 0.4 fusion.44
  4.6 0.7 convolution_convert_fusion
  5.2 0.7 copy.11
  6.0 0.0 copy-start
  6.0 2.3 %reshape.227 = bf16[8,432,160]{2,1,0:T(8,128)(2,1)} reshape(bf16[144,2,12,160]{3,2,1,0:T(8,128)(2,1)S(1)} %copy.11) | data formatting | bytes 2211840 | tf_op jit(solution)/shard_map/reshape | solution.py:122
  8.3 0.0 copy-done
  9.0 1.8 %pad_maximum_fusion = bf16[8,440,160]{2,1,0:T(8,128)(2,1)S(1)} fusion(bf16[8,8,160]{2,1,0:T(8,128)(2,1)S(1)} %broadcast_in_dim.2, bf16[8,432,160]{2,1,0:T(8,128)(2,1)} %reshape.227), kind=kLoop, calls=%fused_computation.1 | loop fusion | flops 2252800 | bytes 2252800 | tf_op jit(solution)/shard_map/concatenate | solution.py:126
  10.8 1.6 %copy.12 = bf16[8,440,160]{1,2,0:T(8,128)(2,1)} copy(bf16[8,440,160]{2,1,0:T(8,128)(2,1)S(1)} %pad_maximum_fusion) | data formatting | bytes 2252800 | tf_op jit(solution)/shard_map/concatenate | solution.py:126
  12.4 7.4 %all-to-all-start = ((bf16[8,440,160]{1,2,0:T(8,128)(2,1)}), bf16[8,440,160]{1,2,0:T(8,128)(2,1)S(1)}, u32[]{:S(2)}, u32[]{:S(2)}) async-start(bf16[8,440,160]{1,2,0:T(8,128)(2,1)} %copy.12), calls=%async_computation | async-start | bytes 2621440 | tf_op jit(solution)/shard_map/all_to_all | solution.py:129
  19.9 0.3 fusion.32
  20.2 0.4 fusion.37
  20.6 0.3 negate_convert_fusion
  20.9 0.8 fusion.15.col_tab
  21.7 0.4 fusion.38
  22.1 0.7 fusion.12.row_tab
  22.7 0.5 broadcast_multiply_fusion.weights
  23.3 28.0 %all-to-all-done = bf16[8,440,160]{1,2,0:T(8,128)(2,1)S(1)} async-done(((bf16[8,440,160]{1,2,0:T(8,128)(2,1)}), bf16[8,440,160]{1,2,0:T(8,128)(2,1)S(1)}, u32[]{:S(2)}, u32[]{:S(2)}) %all-to-all-start) | async-done | bytes 1126432 | tf_op jit(solution)/shard_map/all_to_all | solution.py:129
  51.3 1.7 %copy.13.recv = bf16[8,440,160]{2,1,0:T(8,128)(2,1)} copy(bf16[8,440,160]{1,2,0:T(8,128)(2,1)S(1)} %all-to-all-done) | data formatting | bytes 2252800 | tf_op jit(solution)/shard_map/all_to_all | solution.py:129
  53.0 34.9 %grid.1 = bf16[4,18,36,144]{3,2,1,0:T(8,128)(2,1)} custom-call(f32[12]{0:T(128)} %broadcast_multiply_fusion.weights, bf16[8,440,160]{2,1,0:T(8,128)(2,1)} %copy.13.recv, bf16[80,1024]{1,0:T(8,128)(2,1)} %fusion.12.row_tab, bf16[288,160]{1,0:T(8,128)(2,1)} %fusion.15.col_tab), custom_call_target="tpu_custom_call" | custom-call | tf_op jit(solution)/shard_map/grid/pallas_call | solution.py:132
  87.9 22.5 %all_to_all.10 = bf16[4,18,36,144]{3,2,1,0:T(8,128)(2,1)S(1)} all-to-all(bf16[4,18,36,144]{3,2,1,0:T(8,128)(2,1)} %grid.1), channel_id=1, replica_groups=mesh['fft'=8,'band'=4] {'band'}, dimensions={0} | all-to-all | bytes 1492992 | tf_op jit(solution)/shard_map/all_to_all | solution.py:147
  110.4 1.2 %convert_reduce_fusion = f32[18,36,144]{2,1,0:T(8,128)} fusion(bf16[4,18,36,144]{3,2,1,0:T(8,128)(2,1)S(1)} %all_to_all.10), kind=kLoop, calls=%fused_computation | loop fusion | flops 653184 | bytes 1119744 | tf_op jit(solution)/shard_map/reduce_sum | solution.py:148
  (11 shorter events, 0.1 us)
Async XLA Ops:
  6.0 2.3 %copy-start = (s32[160]{0:T(256)S(1)}, s32[160]{0:T(256)}, u32[]{:S(2)}) copy-start(s32[160]{0:T(256)} %param.7) | copy-start | bytes 1924
  12.4 10.3 %copy-start.1 = (f32[12]{0:T(128)S(1)}, f32[12]{0:T(128)}, u32[]{:S(2)}) copy-start(f32[12]{0:T(128)} %param.6) | copy-start | bytes 148
  12.4 38.8 %all-to-all-start = ((bf16[8,440,160]{1,2,0:T(8,128)(2,1)}), bf16[8,440,160]{1,2,0:T(8,128)(2,1)S(1)}, u32[]{:S(2)}, u32[]{:S(2)}) async-start(bf16[8,440,160]{1,2,0:T(8,128)(2,1)} %copy.12), calls=%async_computation | async-start | bytes 2621440 | tf_op jit(solution)/shard_map/all_to_all | solution.py:129

commit v2 on v1

v2 whole, which is shorter than its diff:
```python
import functools
import math

import jax
import jax.numpy as jnp
import numpy as np
from jax import lax
from jax.experimental import pallas as pl
from jax.experimental.pallas import tpu as pltpu
from jax.sharding import PartitionSpec as P

N = 144
GB = 72
HALF = N // 2
LIVE_PER_DEVICE = 64
GP = 80
LANES = 128
META = 16
MESH = pl.DeviceIdType.MESH


def phase_pair(freq_count, positions, grid):
    freqs = jnp.arange(freq_count, dtype=jnp.int32) - freq_count // 2
    turns = jnp.mod(freqs[:, None] * positions[None, :], grid)
    angles = turns.astype(jnp.float32) * (2.0 * math.pi / grid)
    return (jnp.cos(angles), jnp.sin(angles))


def stick_table(plane_slot):
    valid_slot = (plane_slot >= 0).astype(jnp.float32)
    cosine, sine_part = phase_pair(GB, jnp.maximum(plane_slot, 0), N)
    cosine = cosine * valid_slot[None, :]
    sine_part = sine_part * valid_slot[None, :]
    upper = jnp.stack([cosine, sine_part], axis=-1)
    lower = jnp.stack([-sine_part, cosine], axis=-1)
    return jnp.concatenate([upper, lower], axis=0).astype(jnp.bfloat16)


def fixed_phases():
    freqs = np.arange(GB, dtype=np.int64) - GB // 2
    turns = np.mod(freqs[:, None] * np.arange(N)[None, :], N)
    angles = turns * (2.0 * math.pi / N)
    return np.cos(angles), np.sin(angles)


def row_table():
    cosine, sine_part = fixed_phases()
    table = np.zeros((GP, 2 * LANES))
    table[:GB, : HALF + 1] = cosine[:, : HALF + 1]
    table[:GB, LANES : LANES + HALF + 1] = sine_part[:, : HALF + 1]
    return jnp.asarray(table.astype(jnp.bfloat16))


def column_table():
    cosine, sine_part = fixed_phases()
    table = np.zeros((2 * N, 2 * GP))
    table[:N, :GB] = cosine.T
    table[:N, GP : GP + GB] = -sine_part.T
    table[N:, :GB] = sine_part.T
    table[N:, GP : GP + GB] = cosine.T
    return jnp.asarray(table.astype(jnp.bfloat16))


def order_table():
    table = np.zeros((2 * LANES, N))
    for y in range(N):
        table[y if y <= HALF else LANES + N - y, y] = 1.0
    return jnp.asarray(table.astype(jnp.bfloat16))


def grid_kernel(
    bands, live, chunk_planes, ways, groups,
    weights, outgoing, meta_out, row_tab, col_tab, order,
    out,
    recv, meta_in, sticks, table, masked, row_hot, sent, landed,
    meta_send, meta_recv, go_send, go_recv, sum_send, sum_recv,
):
    plane = pl.program_id(0)
    planes = pl.num_programs(0)
    total_planes = out.shape[0]
    chunks = total_planes // chunk_planes
    chunk_rows = chunk_planes * 2 * bands
    here = recv.shape[-1]
    me = lax.axis_index("fft")
    group = lax.axis_index("band")

    def meta_copy(step, source):
        peer = lax.rem(me + step, ways)
        return pltpu.make_async_remote_copy(
            src_ref=meta_out, dst_ref=meta_in.at[source],
            send_sem=meta_send.at[step - 1], recv_sem=meta_recv.at[source],
            device_id={"fft": peer}, device_id_type=MESH,
        )

    def stick_copy(chunk, step, source):
        peer = lax.rem(me + step, ways)
        return pltpu.make_async_remote_copy(
            src_ref=outgoing.at[peer, pl.ds(chunk * chunk_rows, chunk_rows)],
            dst_ref=recv.at[chunk, source],
            send_sem=go_send.at[chunk, step - 1], recv_sem=go_recv.at[chunk, source],
            device_id={"fft": peer}, device_id_type=MESH,
        )

    def sum_copy(which, step, source):
        peer = lax.rem(group + step, groups)
        return pltpu.make_async_remote_copy(
            src_ref=sent.at[peer, which], dst_ref=landed.at[source, which],
            send_sem=sum_send.at[which, step - 1], recv_sem=sum_recv.at[which, source],
            device_id={"band": peer}, device_id_type=MESH,
        )

    @pl.when(plane == 0)
    def _():
        barrier = pltpu.get_barrier_semaphore()
        for step in range(1, ways):
            pl.semaphore_signal(
                barrier, inc=1, device_id={"fft": lax.rem(me + step, ways)}, device_id_type=MESH
            )
        for step in range(1, groups):
            pl.semaphore_signal(
                barrier, inc=1, device_id={"band": lax.rem(group + step, groups)},
                device_id_type=MESH,
            )
        pl.semaphore_wait(barrier, ways + groups - 2)
        for step in range(1, ways):
            meta_copy(step, me).start()
        for chunk in range(chunks):
            for step in range(1, ways):
                stick_copy(chunk, step, me).start()
        meta_in[me] = meta_out[...]
        for chunk in range(chunks):
            recv[chunk, me] = outgoing[me, chunk * chunk_rows : (chunk + 1) * chunk_rows]
        for step in range(1, ways):
            meta_copy(step, lax.rem(me + ways - step, ways)).wait()

    @pl.when(lax.rem(plane, chunk_planes) == 0)
    def _():
        chunk = plane // chunk_planes
        for step in range(1, ways):
            stick_copy(chunk, step, lax.rem(me + ways - step, ways)).wait()
        offset = jnp.zeros((1, 1), jnp.float32)
        target = lax.broadcasted_iota(jnp.int32, (live, here), 0).astype(jnp.float32)
        place = lax.broadcasted_iota(jnp.int32, (1, here), 1).astype(jnp.float32)
        total = jnp.zeros((chunk_rows, live), jnp.float32)
        facts = jnp.zeros((META, live), jnp.float32)
        for source in range(ways):
            meta = meta_in[source]
            alive = meta.astype(jnp.float32)[2:3, :]
            spot = jnp.where(alive > 0.5, place + offset, -1.0)
            pick = jnp.where(target == spot, 1.0, 0.0).astype(jnp.bfloat16)
            turn = (((1,), (1,)), ((), ()))
            total += lax.dot_general(
                recv[chunk, source], pick, turn, preferred_element_type=jnp.float32
            )
            facts += lax.dot_general(meta, pick, turn, preferred_element_type=jnp.float32)
            offset += jnp.sum(alive, axis=1, keepdims=True)
        sticks[...] = total.reshape(sticks.shape)

        @pl.when(plane == 0)
        def _():
            freq = lax.broadcasted_iota(jnp.int32, (GP, live), 0).astype(jnp.float32)
            row_hot[...] = jnp.where(freq == facts[0:1, :], 1.0, 0.0)
            col_hot = jnp.where(freq == facts[1:2, :], 1.0, 0.0).astype(jnp.bfloat16)
            table[...] = lax.dot_general(
                col_hot, row_tab[...], (((0,), (0,)), ((), ())),
                preferred_element_type=jnp.float32,
            ).astype(jnp.bfloat16)

    mine = sticks[lax.rem(plane, chunk_planes)]
    hot = row_hot[...]
    for index in range(2 * bands):
        masked[index * GP : (index + 1) * GP, :] = (hot * mine[index : index + 1, :]).astype(
            jnp.bfloat16
        )
    made = jnp.dot(masked[...], table[...], preferred_element_type=jnp.float32)
    density = jnp.zeros((N, 2 * LANES), jnp.float32)
    for band in range(bands):
        real_in = made[band * GP : (band + 1) * GP]
        imag_in = made[(bands + band) * GP : (bands + band + 1) * GP]
        rc, rs = real_in[:, :LANES], real_in[:, LANES:]
        ic, im = imag_in[:, :LANES], imag_in[:, LANES:]
        stacked = jnp.concatenate(
            [
                jnp.concatenate([rc - im, rc + im], axis=1),
                jnp.concatenate([ic + rs, ic - rs], axis=1),
            ],
            axis=0,
        ).astype(jnp.bfloat16)
        wave = jnp.dot(col_tab[...], stacked, preferred_element_type=jnp.float32)
        real, imag = wave[:N], wave[N:]
        density += weights[band] * (real * real + imag * imag)
    ordered = jnp.dot(
        density.astype(jnp.bfloat16), order[...], preferred_element_type=jnp.float32
    ).astype(jnp.bfloat16)
    own_rows = N // groups
    for owner in range(groups):
        sent[owner, plane] = ordered[owner * own_rows : (owner + 1) * own_rows]
    for step in range(1, groups):
        sum_copy(plane, step, group).start()

    @pl.when(plane == planes - 1)
    def _():
        def finish(which, carry):
            for step in range(1, groups):
                sum_copy(which, step, lax.rem(group + groups - step, groups)).wait()
            total = sent[group, which].astype(jnp.float32)
            for step in range(1, groups):
                total += landed[lax.rem(group + step, groups), which].astype(jnp.float32)
            out[which] = total
            return carry

        lax.fori_loop(0, total_planes, finish, 0)


def shards(coefficients, occupations, columns, counts, plane_slot):
    bands = coefficients.shape[0]
    here = columns.shape[0]
    ways = lax.axis_size("fft")
    groups = lax.axis_size("band")
    planes = plane_slot.shape[0] // ways
    live = LIVE_PER_DEVICE * ways
    coefficients = coefficients.reshape(bands, here, 2 * GB)
    plane_tab = stick_table(plane_slot)
    weights = occupations / (bands * groups)
    outgoing = jnp.einsum(
        "gjc,bsg->jcbs", plane_tab, coefficients, preferred_element_type=jnp.float32
    ).astype(jnp.bfloat16)
    outgoing = outgoing.reshape(ways, planes * 2 * bands, here)
    alive = jnp.arange(here, dtype=jnp.int32) < counts[0]
    meta = jnp.stack([columns // GB, columns % GB, alive.astype(jnp.int32)]).astype(jnp.bfloat16)
    meta = jnp.pad(meta, ((0, META - 3), (0, 0)))
    rows = N // groups
    chunk_planes = 6 if planes % 6 == 0 else planes
    chunks = planes // chunk_planes
    chunk_rows = chunk_planes * 2 * bands
    whole = pl.BlockSpec(memory_space=pltpu.VMEM)
    dma = pltpu.SemaphoreType.DMA
    return pl.pallas_call(
        functools.partial(grid_kernel, bands, live, chunk_planes, ways, groups),
        grid=(planes,),
        in_specs=[pl.BlockSpec(memory_space=pltpu.SMEM)] + [whole] * 5,
        out_specs=whole,
        out_shape=jax.ShapeDtypeStruct((planes, rows, N), jnp.float32),
        scratch_shapes=[
            pltpu.VMEM((chunks, ways, chunk_rows, here), jnp.bfloat16),
            pltpu.VMEM((ways, META, here), jnp.bfloat16),
            pltpu.VMEM((chunk_planes, 2 * bands, live), jnp.float32),
            pltpu.VMEM((live, 2 * LANES), jnp.bfloat16),
            pltpu.VMEM((2 * bands * GP, live), jnp.bfloat16),
            pltpu.VMEM((GP, live), jnp.float32),
            pltpu.VMEM((groups, planes, rows, N), jnp.bfloat16),
            pltpu.VMEM((groups, planes, rows, N), jnp.bfloat16),
            dma((ways - 1,)),
            dma((ways,)),
            dma((chunks, ways - 1)),
            dma((chunks, ways)),
            dma((planes, groups - 1)),
            dma((planes, groups)),
        ],
        compiler_params=pltpu.CompilerParams(
            vmem_limit_bytes=60 * 1024 * 1024, collective_id=0, has_side_effects=True
        ),
        name="grid",
    )(weights, outgoing, meta, row_table(), column_table(), order_table())


def solution(mesh):
    placed = (P("band", "fft"), P("band"), P("fft"), P("fft"), P())
    return jax.shard_map(
        shards, mesh=mesh, in_specs=placed, out_specs=P("fft", "band", None), check_vma=False
    )
```

time: 112 us -> 94.3 us (0.84)
  the two profiles are of different devices: /device:TPU:0 before, /device:TPU:13 now
where the time goes in v2:
time: 94.3 us; the launch traced here: 94 us
  Pallas kernels  81.8 us (87%)
  local copies, waits for them, and re-layouts  7.9 us (8%)
  other arithmetic  2.91 us (3%)
    pallas_call x1, Pallas kernels, shards(): pl.pallas_call(functools.partial(grid_kernel, bands, live, chunk_planes,...  81.8 us
    reshape x1, local copies, waits for them, and re-layouts, shards(): coefficients = coefficients.reshape(bands, here, 2 * GB)  2.81 us
    reshape x1, local copies, waits for them, and re-layouts, shards(): outgoing = outgoing.reshape(ways, planes * 2 * bands, here)  2.3 us
    unnamed x5, local copies, waits for them, and re-layouts  2.04 us

profile of v2, /device:TPU:13, one launch (start us, length us, event | category | flops | bytes accessed | tf_op | source)
XLA Modules:
  0.0 94.0 jit_solution(16174941688659662524)
XLA Ops:
  0.0 0.7 broadcast_maximum_fusion
  0.7 0.7 compare_convert_fusion.1
  1.4 0.4 fusion.12
  1.8 2.8 %reshape.225 = bf16[12,160,144]{2,1,0:T(8,128)(2,1)S(1)} reshape(bf16[12,23040]{1,0:T(8,128)(2,1)} %param.8) | data formatting | bytes 1105920 | tf_op jit(solution)/shard_map/reshape | solution.py:222
  4.6 0.7 convolution_convert_fusion
  5.2 0.7 copy.12
  6.0 0.0 copy-start
  6.0 0.0 copy-start.1
  6.0 2.3 %reshape.226.outgoing = bf16[8,432,160]{2,1,0:T(8,128)(2,1)} reshape(bf16[144,2,12,160]{3,2,1,0:T(8,128)(2,1)S(1)} %copy.12) | data formatting | bytes 2211840 | tf_op jit(solution)/shard_map/reshape | solution.py:228
  8.3 0.0 copy-done
  9.0 0.6 fusion.17.meta_out
  9.6 0.0 copy-done.1
  9.6 0.5 broadcast_multiply_fusion.weights
  10.2 81.8 %grid.1 = f32[18,36,144]{2,1,0:T(8,128)} custom-call(f32[12]{0:T(128)} %broadcast_multiply_fusion.weights, bf16[8,432,160]{2,1,0:T(8,128)(2,1)} %reshape.226.outgoing, bf16[16,160]{1,0:T(8,128)(2,1)} %fusion.17.meta_out, bf16[80,256]{1,0:T(8,128)(2,1)} %constant.49.clone.row_tab, bf16[288,160]{1,0:T(8,128)(2,1)} %constant.50.clone.col_tab, ...), custom_call_target="tpu_custom_call" | custom-call | tf_op jit(solution)/shard_map/grid/pallas_call | solution.py:238
  92.0 2.0 %copy.18 = f32[18,36,144]{2,1,0:T(8,128)} copy(f32[18,36,144]{2,1,0:T(8,128)} %grid.1) | data formatting | bytes 746496
  (5 shorter events, 0.0 us)
Async XLA Ops:
  6.0 2.3 %copy-start = (s32[160]{0:T(256)S(1)}, s32[160]{0:T(256)}, u32[]{:S(2)}) copy-start(s32[160]{0:T(256)} %param.10) | copy-start | bytes 1924
  6.0 3.6 %copy-start.1 = (f32[12]{0:T(128)S(1)}, f32[12]{0:T(128)}, u32[]{:S(2)}) copy-start(f32[12]{0:T(128)} %param.9) | copy-start | bytes 148

commit v3 on v2

--- a/solution.py
+++ b/solution.py
@@ -11,10 +11,9 @@
 
 N = 144
 GB = 72
-HALF = N // 2
 LIVE_PER_DEVICE = 64
 GP = 80
-LANES = 128
+YP = 256
 META = 16
 MESH = pl.DeviceIdType.MESH
 
@@ -45,10 +44,10 @@
 
 def row_table():
     cosine, sine_part = fixed_phases()
-    table = np.zeros((GP, 2 * LANES))
-    table[:GB, : HALF + 1] = cosine[:, : HALF + 1]
-    table[:GB, LANES : LANES + HALF + 1] = sine_part[:, : HALF + 1]
-    return jnp.asarray(table.astype(jnp.bfloat16))
+    table = np.zeros((GP, 4, YP))
+    for place, part in enumerate((cosine, sine_part, -sine_part, cosine)):
+        table[:GB, place, :N] = part
+    return jnp.asarray(table.reshape(GP, 4 * YP).astype(jnp.bfloat16))
 
 
 def column_table():
@@ -61,18 +60,11 @@
     return jnp.asarray(table.astype(jnp.bfloat16))
 
 
-def order_table():
-    table = np.zeros((2 * LANES, N))
-    for y in range(N):
-        table[y if y <= HALF else LANES + N - y, y] = 1.0
-    return jnp.asarray(table.astype(jnp.bfloat16))
-
-
 def grid_kernel(
     bands, live, chunk_planes, ways, groups,
-    weights, outgoing, meta_out, row_tab, col_tab, order,
+    weights, outgoing, meta_out, row_tab, col_tab,
     out,
-    recv, meta_in, sticks, table, masked, row_hot, sent, landed,
+    recv, meta_in, picks, sticks, table, masked, row_hot, sent, landed,
     meta_send, meta_recv, go_send, go_recv, sum_send, sum_recv,
 ):
     plane = pl.program_id(0)
@@ -138,60 +130,58 @@
         chunk = plane // chunk_planes
         for step in range(1, ways):
             stick_copy(chunk, step, lax.rem(me + ways - step, ways)).wait()
-        offset = jnp.zeros((1, 1), jnp.float32)
-        target = lax.broadcasted_iota(jnp.int32, (live, here), 0).astype(jnp.float32)
-        place = lax.broadcasted_iota(jnp.int32, (1, here), 1).astype(jnp.float32)
-        total = jnp.zeros((chunk_rows, live), jnp.float32)
-        facts = jnp.zeros((META, live), jnp.float32)
-        for source in range(ways):
-            meta = meta_in[source]
-            alive = meta.astype(jnp.float32)[2:3, :]
-            spot = jnp.where(alive > 0.5, place + offset, -1.0)
-            pick = jnp.where(target == spot, 1.0, 0.0).astype(jnp.bfloat16)
-            turn = (((1,), (1,)), ((), ()))
-            total += lax.dot_general(
-                recv[chunk, source], pick, turn, preferred_element_type=jnp.float32
-            )
-            facts += lax.dot_general(meta, pick, turn, preferred_element_type=jnp.float32)
-            offset += jnp.sum(alive, axis=1, keepdims=True)
-        sticks[...] = total.reshape(sticks.shape)
+        turn = (((1,), (1,)), ((), ()))
 
         @pl.when(plane == 0)
         def _():
+            offset = jnp.zeros((1, 1), jnp.float32)
+            target = lax.broadcasted_iota(jnp.int32, (live, here), 0).astype(jnp.float32)
+            place = lax.broadcasted_iota(jnp.int32, (1, here), 1).astype(jnp.float32)
+            facts = jnp.zeros((META, live), jnp.float32)
+            for source in range(ways):
+                meta = meta_in[source]
+                alive = meta.astype(jnp.float32)[2:3, :]
+                spot = jnp.where(alive > 0.5, place + offset, -1.0)
+                pick = jnp.where(target == spot, 1.0, 0.0).astype(jnp.bfloat16)
+                picks[source] = pick
+                facts += lax.dot_general(meta, pick, turn, preferred_element_type=jnp.float32)
+                offset += jnp.sum(alive, axis=1, keepdims=True)
             freq = lax.broadcasted_iota(jnp.int32, (GP, live), 0).astype(jnp.float32)
             row_hot[...] = jnp.where(freq == facts[0:1, :], 1.0, 0.0)
             col_hot = jnp.where(freq == facts[1:2, :], 1.0, 0.0).astype(jnp.bfloat16)
-            table[...] = lax.dot_general(
-                col_hot, row_tab[...], (((0,), (0,)), ((), ())),
-                preferred_element_type=jnp.float32,
-            ).astype(jnp.bfloat16)
+            for part in range(2):
+                table[part * live : (part + 1) * live, :] = lax.dot_general(
+                    col_hot,
+                    row_tab[:, 2 * YP * part : 2 * YP * (part + 1)],
+                    (((0,), (0,)), ((), ())),
+                    preferred_element_type=jnp.float32,
+                ).astype(jnp.bfloat16)
+
+        total = jnp.zeros((chunk_rows, live), jnp.float32)
+        for source in range(ways):
+            total += lax.dot_general(
+                recv[chunk, source], picks[source], turn, preferred_element_type=jnp.float32
+            )
+        sticks[...] = total.reshape(sticks.shape)
 
     mine = sticks[lax.rem(plane, chunk_planes)]
     hot = row_hot[...]
-    for index in range(2 * bands):
-        masked[index * GP : (index + 1) * GP, :] = (hot * mine[index : index + 1, :]).astype(
-            jnp.bfloat16
-        )
-    made = jnp.dot(masked[...], table[...], preferred_element_type=jnp.float32)
-    density = jnp.zeros((N, 2 * LANES), jnp.float32)
+    for part in range(2):
+        for band in range(bands):
+            row = mine[part * bands + band : part * bands + band + 1, :]
+            masked[band * GP : (band + 1) * GP, part * live : (part + 1) * live] = (
+                hot * row
+            ).astype(jnp.bfloat16)
+    half = jnp.dot(masked[...], table[...], preferred_element_type=jnp.float32)
+    half = half.astype(jnp.bfloat16)
+    density = jnp.zeros((N, YP), jnp.float32)
     for band in range(bands):
-        real_in = made[band * GP : (band + 1) * GP]
-        imag_in = made[(bands + band) * GP : (bands + band + 1) * GP]
-        rc, rs = real_in[:, :LANES], real_in[:, LANES:]
-        ic, im = imag_in[:, :LANES], imag_in[:, LANES:]
-        stacked = jnp.concatenate(
-            [
-                jnp.concatenate([rc - im, rc + im], axis=1),
-                jnp.concatenate([ic + rs, ic - rs], axis=1),
-            ],
-            axis=0,
-        ).astype(jnp.bfloat16)
+        piece = half[band * GP : (band + 1) * GP, :]
+        stacked = jnp.concatenate([piece[:, :YP], piece[:, YP:]], axis=0)
         wave = jnp.dot(col_tab[...], stacked, preferred_element_type=jnp.float32)
         real, imag = wave[:N], wave[N:]
         density += weights[band] * (real * real + imag * imag)
-    ordered = jnp.dot(
-        density.astype(jnp.bfloat16), order[...], preferred_element_type=jnp.float32
-    ).astype(jnp.bfloat16)
+    ordered = density[:, :N].astype(jnp.bfloat16)
     own_rows = N // groups
     for owner in range(groups):
         sent[owner, plane] = ordered[owner * own_rows : (owner + 1) * own_rows]
@@ -238,15 +228,16 @@
     return pl.pallas_call(
         functools.partial(grid_kernel, bands, live, chunk_planes, ways, groups),
         grid=(planes,),
-        in_specs=[pl.BlockSpec(memory_space=pltpu.SMEM)] + [whole] * 5,
+        in_specs=[pl.BlockSpec(memory_space=pltpu.SMEM)] + [whole] * 4,
         out_specs=whole,
         out_shape=jax.ShapeDtypeStruct((planes, rows, N), jnp.float32),
         scratch_shapes=[
             pltpu.VMEM((chunks, ways, chunk_rows, here), jnp.bfloat16),
             pltpu.VMEM((ways, META, here), jnp.bfloat16),
+            pltpu.VMEM((ways, live, here), jnp.bfloat16),
             pltpu.VMEM((chunk_planes, 2 * bands, live), jnp.float32),
-            pltpu.VMEM((live, 2 * LANES), jnp.bfloat16),
-            pltpu.VMEM((2 * bands * GP, live), jnp.bfloat16),
+            pltpu.VMEM((2 * live, 2 * YP), jnp.bfloat16),
+            pltpu.VMEM((bands * GP, 2 * live), jnp.bfloat16),
             pltpu.VMEM((GP, live), jnp.float32),
             pltpu.VMEM((groups, planes, rows, N), jnp.bfloat16),
             pltpu.VMEM((groups, planes, rows, N), jnp.bfloat16),
@@ -261,7 +252,7 @@
             vmem_limit_bytes=60 * 1024 * 1024, collective_id=0, has_side_effects=True
         ),
         name="grid",
-    )(weights, outgoing, meta, row_table(), column_table(), order_table())
+    )(weights, outgoing, meta, row_table(), column_table())
 
 
 def solution(mesh):

time: 94.3 us -> 86.2 us (0.914)
  Pallas kernels: 81.8 us -> 73.7 us
    pallas_call x1, Pallas kernels: 81.8 us -> 73.7 us  [shards(): pl.pallas_call(functools.partial(grid_kernel, bands, live, chunk_planes,...]
where the time goes in v3:
time: 86.2 us; the launch traced here: 85.9 us
  Pallas kernels  73.7 us (85%)
  local copies, waits for them, and re-layouts  7.9 us (9%)
  other arithmetic  2.91 us (3%)
    pallas_call x1, Pallas kernels, shards(): pl.pallas_call(functools.partial(grid_kernel, bands, live, chunk_planes,...  73.7 us
    reshape x1, local copies, waits for them, and re-layouts, shards(): coefficients = coefficients.reshape(bands, here, 2 * GB)  2.81 us
    reshape x1, local copies, waits for them, and re-layouts, shards(): outgoing = outgoing.reshape(ways, planes * 2 * bands, here)  2.3 us
    unnamed x5, local copies, waits for them, and re-layouts  2.04 us

profile of v3, /device:TPU:13, one launch (start us, length us, event | category | flops | bytes accessed | tf_op | source)
XLA Modules:
  0.0 85.9 jit_solution(8402783363267201119)
XLA Ops:
  0.0 0.7 broadcast_maximum_fusion
  0.7 0.7 compare_convert_fusion.1
  1.4 0.4 fusion.12
  1.8 2.8 %reshape.225 = bf16[12,160,144]{2,1,0:T(8,128)(2,1)S(1)} reshape(bf16[12,23040]{1,0:T(8,128)(2,1)} %param.7) | data formatting | bytes 1105920 | tf_op jit(solution)/shard_map/reshape | solution.py:212
  4.6 0.7 convolution_convert_fusion
  5.2 0.7 copy.11
  6.0 0.0 copy-start
  6.0 0.0 copy-start.1
  6.0 2.3 %reshape.226.outgoing = bf16[8,432,160]{2,1,0:T(8,128)(2,1)} reshape(bf16[144,2,12,160]{3,2,1,0:T(8,128)(2,1)S(1)} %copy.11) | data formatting | bytes 2211840 | tf_op jit(solution)/shard_map/reshape | solution.py:218
  8.3 0.0 copy-done
  9.0 0.6 fusion.17.meta_out
  9.6 0.0 copy-done.1
  9.6 0.5 broadcast_multiply_fusion.weights
  10.2 73.7 %grid.1 = f32[18,36,144]{2,1,0:T(8,128)} custom-call(f32[12]{0:T(128)} %broadcast_multiply_fusion.weights, bf16[8,432,160]{2,1,0:T(8,128)(2,1)} %reshape.226.outgoing, bf16[16,160]{1,0:T(8,128)(2,1)} %fusion.17.meta_out, bf16[80,1024]{1,0:T(8,128)(2,1)} %constant.47.clone.row_tab, bf16[288,160]{1,0:T(8,128)(2,1)} %constant.48.clone.col_tab), custom_call_target="tpu_custom_call" | custom-call | tf_op jit(solution)/shard_map/grid/pallas_call | solution.py:228
  83.9 2.0 %copy.17 = f32[18,36,144]{2,1,0:T(8,128)} copy(f32[18,36,144]{2,1,0:T(8,128)} %grid.1) | data formatting | bytes 746496
  (5 shorter events, 0.0 us)
Async XLA Ops:
  6.0 2.3 %copy-start = (s32[160]{0:T(256)S(1)}, s32[160]{0:T(256)}, u32[]{:S(2)}) copy-start(s32[160]{0:T(256)} %param.9) | copy-start | bytes 1924
  6.0 3.6 %copy-start.1 = (f32[12]{0:T(128)S(1)}, f32[12]{0:T(128)}, u32[]{:S(2)}) copy-start(f32[12]{0:T(128)} %param.8) | copy-start | bytes 148
